TPU v7x, 32 devices: a whole 2x2x4 slice. The times are simulated.
32 devices in a mesh: kpt: 2 (over x), row: 8 (over z, y), col: 2 (over core).
Axes of the slice: x: 2, y: 2, z: 4, core: 2. Of those that a mesh axis runs over, the one named last changes fastest.
Arguments:
- wannier: float32 [64, 32, 1024], P('kpt', ('row', 'col')), parts along dimension 0, may hold values from -6 to 6
- pairs: int32 [384, 2], replicated, may hold values from 0 to 31, as said below
- gmap: int32 [8192], replicated, may hold values from 1 to 32767, as said below
- screened: bfloat16 [4, 2, 8192, 8192], P('kpt', None, 'row', 'col'), parts along dimension 0, may hold values from -0.046875 to 0.046875
Outputs:
- coulomb: float32 [2, 2, 768, 384], P(None, None, ('kpt', 'row', 'col')), parts along dimension 2
There are 2 independent parts, one for each index of `kpt`. A program takes and returns all parts, laid end to end along the dimension named above; an argument that names none is the same for every part. Nothing has to cross between parts.
Inputs may be any that keep to these rules, and one draw needn't show every extreme that they name: `gmap`: 8192 distinct flat cells of the grid; cell 0 is never among them. `pairs`: in each row the first Wannier function is no greater than the second; no two rows are equal.
All inputs are finite; a program needn't handle non-finite values.
Results may differ from a plain program's by a relative error of at most 0.0082.
Values may be sent and summed in bfloat16 or wider, within the bound.
No kernel may reach another device: no remote copies, remote signals or barrier semaphores. Data moves between devices by JAX's collectives and lax.ppermute only.
A program may use at most 128 MiB of HBM per device.

v0:
```python
import math
import jax
import jax.numpy as jnp
from jax import lax
from jax.sharding import PartitionSpec as P

NW = 32
GX = 32
NG = 8192
NP = 384


def line_tables(side_len):
    positions = jnp.arange(side_len, dtype=jnp.int32)
    phase_index = positions[:, None] * positions[None, :] % side_len
    angles = phase_index.astype(jnp.float32) * (2.0 * math.pi / side_len)
    return (jnp.cos(angles), jnp.sin(angles))


def plane_transform(density):
    cosine, sine_table = line_tables(GX)
    highest = lax.Precision.HIGHEST
    shaped = density.reshape(-1, GX, GX)
    real_z = jnp.einsum("nyz,kz->nyk", shaped, cosine, precision=highest)
    imag_z = -jnp.einsum("nyz,kz->nyk", shaped, sine_table, precision=highest)
    new_real = jnp.einsum("jy,nyk->njk", cosine, real_z, precision=highest) + jnp.einsum(
        "jy,nyk->njk", sine_table, imag_z, precision=highest
    )
    new_imag = jnp.einsum("jy,nyk->njk", cosine, imag_z, precision=highest) - jnp.einsum(
        "jy,nyk->njk", sine_table, real_z, precision=highest
    )
    return (new_real.reshape(density.shape), new_imag.reshape(density.shape))


def line_transform(real_part, imag_part):
    cosine, sine_table = line_tables(GX)
    highest = lax.Precision.HIGHEST
    new_real = jnp.einsum("kn,pny->pky", cosine, real_part, precision=highest) + jnp.einsum(
        "kn,pny->pky", sine_table, imag_part, precision=highest
    )
    new_imag = jnp.einsum("kn,pny->pky", cosine, imag_part, precision=highest) - jnp.einsum(
        "kn,pny->pky", sine_table, real_part, precision=highest
    )
    return (new_real, new_imag)


def right_columns(screened, segment):
    w_real = screened[:, 0]
    w_imag = screened[:, 1]
    real_real = jnp.einsum("fgh,bh->fgb", w_real, segment[0], preferred_element_type=jnp.float32)
    imag_imag = jnp.einsum("fgh,bh->fgb", w_imag, segment[1], preferred_element_type=jnp.float32)
    real_imag = jnp.einsum("fgh,bh->fgb", w_real, segment[1], preferred_element_type=jnp.float32)
    imag_real = jnp.einsum("fgh,bh->fgb", w_imag, segment[0], preferred_element_type=jnp.float32)
    return jnp.stack([real_real - imag_imag, real_imag + imag_real], axis=1)


def shards(wannier, pairs, gmap, screened):
    planes = wannier.shape[1]
    grid_cells = wannier.shape[2]
    members = jnp.arange(NW, dtype=jnp.int32)[None, :]
    pick_first = (pairs[:, 0:1] == members).astype(jnp.float32)
    pick_second = (pairs[:, 1:2] == members).astype(jnp.float32)
    flat_rows = wannier.reshape(NW, -1)
    highest = lax.Precision.HIGHEST
    density = jnp.dot(pick_first, flat_rows, precision=highest) * jnp.dot(
        pick_second, flat_rows, precision=highest
    )
    density = density.reshape(NP, planes, grid_cells)
    arrived = lax.all_to_all(density, ("row", "col"), split_axis=0, concat_axis=1, tiled=True)
    real_part, imag_part = plane_transform(arrived)
    real_part, imag_part = line_transform(real_part, imag_part)
    owned = real_part.shape[0]
    norm_factor = 1.0 / math.sqrt(GX * GX * GX)
    rho_real = jnp.take(real_part.reshape(owned, -1), gmap, axis=1) * norm_factor
    rho_imag = jnp.take(imag_part.reshape(owned, -1), gmap, axis=1) * norm_factor
    rho = jnp.stack([rho_real, rho_imag], axis=0).astype(jnp.bfloat16)
    row_span = screened.shape[2]
    halves = lax.all_to_all(rho, "col", split_axis=2, concat_axis=1, tiled=True)
    screened_rho = right_columns(screened, lax.all_gather(halves, "row", axis=1, tiled=True))
    blocks = lax.all_to_all(rho, "row", split_axis=2, concat_axis=1, tiled=True)
    blocks = blocks.reshape(2, lax.axis_size("row"), owned, row_span)
    left_panel = lax.all_gather(blocks, "col", axis=2, tiled=True).reshape(2, NP, row_span)
    left_wide = left_panel.astype(jnp.float32)
    u_real = jnp.einsum(
        "ag,fgb->fab", left_wide[0], screened_rho[:, 0], precision=highest
    ) + jnp.einsum("ag,fgb->fab", left_wide[1], screened_rho[:, 1], precision=highest)
    u_imag = jnp.einsum(
        "ag,fgb->fab", left_wide[0], screened_rho[:, 1], precision=highest
    ) - jnp.einsum("ag,fgb->fab", left_wide[1], screened_rho[:, 0], precision=highest)
    partial_terms = jnp.stack([u_real, u_imag], axis=1) / math.sqrt(NG)
    summed = lax.psum(partial_terms, ("row", "col"))
    share_rows = NP // lax.axis_size(("row", "col"))
    return lax.dynamic_slice_in_dim(
        summed, lax.axis_index(("row", "col")) * share_rows, share_rows, 2
    )


def solution(mesh):
    return jax.shard_map(
        shards,
        mesh=mesh,
        in_specs=(P("kpt", ("row", "col"), None), P(), P(), P("kpt", None, "row", "col")),
        out_specs=P(None, None, ("kpt", "row", "col"), None),
        check_vma=False,
    )
```

profile of v0, /device:TPU:0, one launch (start us, length us, event | category | flops | bytes accessed | tf_op | source)
XLA Modules:
  0.0 687.3 jit_solution(8600309741713015094)
XLA Ops:
  6.5 0.8 slice_reduce_fusion
  7.3 1.0 copy.93
  8.3 1.4 fusion.54
  9.8 1.5 convolution_multiply_fusion
  11.3 3.8 reshape.35
  15.1 7.5 %all-to-all-start = ((f32[384,2,1024]{2,1,0:T(2,128)}), f32[384,2,1024]{2,1,0:T(2,128)S(1)}, u32[]{:S(2)}, u32[]{:S(2)}) async-start(f32[384,2,1024]{2,1,0:T(2,128)} %reshape.35), calls=%async_computation | async-start | bytes 6291456 | tf_op jit(solution)/shard_map/all_to_all | solution.py:69
  22.6 0.0 all-gather.5.cloned.1.call-start
  22.7 0.0 copy-done.4
  22.7 59.1 %all-to-all-done = f32[384,2,1024]{2,1,0:T(2,128)S(1)} async-done(((f32[384,2,1024]{2,1,0:T(2,128)}), f32[384,2,1024]{2,1,0:T(2,128)S(1)}, u32[]{:S(2)}, u32[]{:S(2)}) %all-to-all-start) | async-done | bytes 3145760 | tf_op jit(solution)/shard_map/all_to_all | solution.py:69
  81.9 1.0 copy.70
  82.9 2.4 copy.71
  85.3 7.6 %reshape.36 = f32[768,32,32]{2,1,0:T(8,128)} reshape(f32[24,16,2,1024]{3,2,1,0:T(2,128)S(1)} %copy.71) | data formatting | bytes 6291456 | tf_op jit(solution)/shard_map/reshape | solution.py:23
  92.9 9.2 %copy.72 = f32[768,32,32]{0,2,1:T(8,128)S(1)} copy(f32[768,32,32]{2,1,0:T(8,128)} %reshape.36) | data formatting | bytes 6291456 | tf_op jit(solution)/shard_map/reshape | solution.py:23
  102.1 3.0 convolution_negate_fusion
  105.1 3.0 fusion.72
  108.1 4.9 fusion.22
  113.1 5.2 fusion.24
  118.2 6.7 add_bitcast_fusion.1
  125.0 5.5 subtract_bitcast_fusion.1
  130.5 10.6 %copy.79 = f32[768,32,32]{2,1,0:T(8,128)} copy(f32[768,32,32]{0,1,2:T(8,128)S(1)} %subtract_bitcast_fusion.1) | data formatting | bytes 6291456 | tf_op jit(solution)/shard_map/sub | solution.py:29
  141.1 9.4 %reshape.38 = f32[24,32,1024]{2,1,0:T(8,128)S(1)} reshape(f32[768,32,32]{2,1,0:T(8,128)} %copy.79) | data formatting | bytes 6291456 | tf_op jit(solution)/shard_map/reshape | solution.py:32
  150.4 5.5 fusion.66
  155.9 11.4 %copy.76 = f32[768,32,32]{2,1,0:T(8,128)} copy(f32[768,32,32]{0,1,2:T(8,128)} %add_bitcast_fusion.1) | data formatting | bytes 6291456 | tf_op jit(solution)/shard_map/add | solution.py:26
  167.3 10.7 %reshape.37 = f32[24,32,1024]{2,1,0:T(8,128)} reshape(f32[768,32,32]{2,1,0:T(8,128)} %copy.76) | data formatting | bytes 6291456 | tf_op jit(solution)/shard_map/reshape | solution.py:32
  178.0 5.9 fusion.69
  184.0 5.5 subtract_bitcast_fusion
  189.5 5.6 add_bitcast_fusion
  195.1 10.3 %copy.89 = f32[24,32,1024]{0,2,1:T(8,128)} copy(f32[24,32,1024]{2,1,0:T(8,128)} %add_bitcast_fusion) | data formatting | bytes 6291456 | tf_op jit(solution)/shard_map/reshape | solution.py:74
  205.4 0.0 copy-done.2
  205.4 8.6 %copy.90 = f32[24,32,1024]{0,2,1:T(8,128)} copy(f32[24,32,1024]{2,1,0:T(8,128)S(1)} %copy-done.2) | data formatting | bytes 6291456 | tf_op jit(solution)/shard_map/reshape | solution.py:75
  214.0 33.6 %gather_fusion = f32[8192,24]{1,0:T(8,128)} fusion(f32[24,32768]{0,1:T(8,128)} %bitcast.144, s32[8192]{0:T(1024)S(1)} %fusion.57), kind=kCustom, calls=%fused_computation.clone | custom fusion | bytes 1605632 | tf_op jit(solution)/shard_map/jit(_take)/gather | solution.py:74
  247.6 33.6 %gather_fusion.1 = f32[8192,24]{1,0:T(8,128)} fusion(f32[24,32768]{0,1:T(8,128)} %bitcast.143, s32[8192]{0:T(1024)S(1)} %fusion.57), kind=kCustom, calls=%fused_computation.1.clone | custom fusion | bytes 1605632 | tf_op jit(solution)/shard_map/jit(_take)/gather | solution.py:75
  281.3 7.2 %fusion.30 = (bf16[1,24,8192]{1,2,0:T(8,128)(2,1)S(1)}, bf16[1,24,8192]{1,2,0:T(8,128)(2,1)S(1)}) fusion(f32[8192,24]{1,0:T(8,128)} %gather_fusion, pred[8192]{0:T(1024)(128)(4,1)S(1)} %compare_and_fusion, f32[8192,24]{1,0:T(8,128)} %gather_fusion.1), kind=kLoop, calls=%fused_computation.43 | loop fusion | flops 1179648 | bytes 2367488 | tf_op jit(solution)/shard_map/stack | solution.py:76
  288.4 0.9 pad_maximum_fusion
  289.4 35.5 %copy.108 = bf16[2,24,8192]{1,0,2:T(2,128)(2,1)} copy(bf16[2,24,8192]{1,2,0:T(8,128)(2,1)S(1)} %pad_maximum_fusion) | data formatting | bytes 1572864 | tf_op jit(solution)/shard_map/stack | solution.py:76
  324.9 6.6 reshape.71
  331.5 35.8 %all_to_all.48 = bf16[8,2,24576]{2,1,0:T(2,128)(2,1)S(1)} all-to-all(bf16[8,2,24576]{2,1,0:T(2,128)(2,1)S(1)} %reshape.71), channel_id=1, replica_groups=mesh['kpt'=2,'row'=8,'col'=2] {'row'}, dimensions={0} | all-to-all | bytes 1572864 | tf_op jit(solution)/shard_map/all_to_all | solution.py:80
  367.3 6.9 %reshape.72 = bf16[8192,2,24]{2,1,0:T(2,128)(2,1)} reshape(bf16[8,2,24576]{2,1,0:T(2,128)(2,1)S(1)} %all_to_all.48) | data formatting | bytes 1572864
  374.3 10.3 %copy.87 = bf16[2,24,8,1024]{3,1,2,0:T(8,128)(2,1)} copy(bf16[2,24,8,1024]{1,0,3,2:T(2,128)(2,1)} %bitcast.145) | data formatting | bytes 1572864 | tf_op jit(solution)/shard_map/all_to_all | solution.py:80
  384.6 0.0 all-gather.5.cloned.1.call-update
  384.6 0.0 all-gather.3.cloned.1.call-start
  384.6 10.2 %copy.109 = bf16[2,24,8192]{1,0,2:T(2,128)(2,1)} copy(bf16[2,24,8192]{1,2,0:T(8,128)(2,1)} %copy-done) | data formatting | bytes 1572864 | tf_op jit(solution)/shard_map/stack | solution.py:76
  394.8 7.0 %reshape.73 = bf16[2,2,98304]{2,1,0:T(2,128)(2,1)S(1)} reshape(bf16[8192,2,24]{2,1,0:T(2,128)(2,1)} %bitcast.147) | data formatting | bytes 1572864
  401.9 4.4 all_to_all.49
  406.2 7.3 %reshape.74 = bf16[8192,2,24]{2,1,0:T(2,128)(2,1)} reshape(bf16[2,2,98304]{2,1,0:T(2,128)(2,1)S(1)} %all_to_all.49) | data formatting | bytes 1572864
  413.6 9.5 %copy.83 = bf16[2,24,2,4096]{3,1,2,0:T(8,128)(2,1)} copy(bf16[2,24,2,4096]{1,0,3,2:T(2,128)(2,1)} %bitcast.146) | data formatting | bytes 1572864 | tf_op jit(solution)/shard_map/all_to_all | solution.py:78
  423.0 0.0 all-gather.3.cloned.1.call-update
  423.1 0.0 all-reduce.2.cloned.1.call-start
  423.1 0.0 all-gather.5.cloned.1.call-done
  423.1 1.5 fusion.129
  424.7 96.3 %all-gather.3.cloned.1.call-done = bf16[2,384,4096]{2,1,0:T(8,128)(2,1)} async-done(((bf16[2,48,4096]{2,1,0:T(8,128)(2,1)}), bf16[2,384,4096]{2,1,0:T(8,128)(2,1)}) %all-gather.3.cloned.1.call-update) | async-done | bytes 6291472 | tf_op jit(solution)/shard_map/all_gather | solution.py:79
  521.0 11.4 %fusion = f32[384,2,1024]{2,0,1:T(8,128)S(1)} fusion(bf16[2,2,1024,4096]{3,2,1,0:T(8,128)(2,1)} %param.9, bf16[2,384,4096]{2,1,0:T(8,128)(2,1)} %all-gather.3.cloned.1.call-done), kind=kOutput, calls=%fused_computation.2 | convolution fusion | flops 6442450944 | bytes 23068672 | tf_op jit(solution)/shard_map/fgh,bh->fgb/dot_general | solution.py:53
  532.4 11.2 %fusion.39 = f32[384,2,1024]{2,0,1:T(8,128)S(1)} fusion(f32[384,2,1024]{2,0,1:T(8,128)S(1)} %fusion, bf16[2,2,1024,4096]{3,2,1,0:T(8,128)(2,1)} %param.9, bf16[2,384,4096]{2,1,0:T(8,128)(2,1)} %all-gather.3.cloned.1.call-done), kind=kOutput, calls=%fused_computation.47 | convolution fusion | flops 6443237376 | bytes 26214400 | tf_op jit(solution)/shard_map/fgh,bh->fgb/dot_general | solution.py:52
  543.6 2.6 fusion.14
  546.2 2.6 fusion.16
  548.9 12.6 %fusion.2 = f32[384,2,1024]{2,0,1:T(8,128)} fusion(bf16[2,2,1024,4096]{3,2,1,0:T(8,128)(2,1)} %param.9, bf16[2,384,4096]{2,1,0:T(8,128)(2,1)} %all-gather.3.cloned.1.call-done), kind=kOutput, calls=%fused_computation.4 | convolution fusion | flops 6442450944 | bytes 23068672 | tf_op jit(solution)/shard_map/fgh,bh->fgb/dot_general | solution.py:51
  561.5 12.1 %fusion.36 = f32[384,2,1024]{2,0,1:T(8,128)S(1)} fusion(f32[384,2,1024]{2,0,1:T(8,128)} %fusion.2, bf16[2,2,1024,4096]{3,2,1,0:T(8,128)(2,1)} %param.9, bf16[2,384,4096]{2,1,0:T(8,128)(2,1)} %all-gather.3.cloned.1.call-done), kind=kOutput, calls=%fused_computation.46 | convolution fusion | flops 6443237376 | bytes 26214400 | tf_op jit(solution)/shard_map/fgh,bh->fgb/dot_general | solution.py:50
  573.6 2.7 fusion.48
  576.3 2.7 fusion.51
  579.0 1.6 maximum_multiply_fusion
  580.6 0.0 all-reduce.2.cloned.1.call-update
  580.6 97.4 %all-reduce.2.cloned.1.call-done = f32[2,2,384,384]{2,3,0,1:T(8,128)} async-done(((f32[2,2,384,384]{2,3,0,1:T(8,128)}), f32[2,2,384,384]{2,3,0,1:T(8,128)}) %all-reduce.2.cloned.1.call-update) | async-done | bytes 2359312 | tf_op jit(solution)/shard_map/psum | solution.py:91
  678.0 1.7 constant_dynamic-slice_fusion
  679.6 0.9 copy.88
  (10 shorter events, 0.0 us)
Async XLA Ops:
  15.1 7.6 %copy-start.4 = (s32[8192]{0:T(1024)S(1)}, s32[8192]{0:T(1024)}, u32[]{:S(2)}) copy-start(s32[8192]{0:T(1024)} %param.8) | copy-start | bytes 98308
  15.1 66.8 %all-to-all-start = ((f32[384,2,1024]{2,1,0:T(2,128)}), f32[384,2,1024]{2,1,0:T(2,128)S(1)}, u32[]{:S(2)}, u32[]{:S(2)}) async-start(f32[384,2,1024]{2,1,0:T(2,128)} %reshape.35), calls=%async_computation | async-start | bytes 6291456 | tf_op jit(solution)/shard_map/all_to_all | solution.py:69
  22.6 400.5 %all-gather.5.cloned.1.call-start = ((), (), s32[]{:S(2)}) async-start(), calls=%async_computation.4 | async-start | bytes 2359296 | tf_op jit(solution)/shard_map/all_gather | solution.py:82
  178.0 6.0 copy-start.1
  178.0 6.0 copy-start.3
  195.1 10.3 %copy-start.2 = (f32[24,32,1024]{2,1,0:T(8,128)S(1)}, f32[24,32,1024]{2,1,0:T(8,128)}, u32[]{:S(2)}) copy-start(f32[24,32,1024]{2,1,0:T(8,128)} %subtract_bitcast_fusion) | copy-start | bytes 9437188
  289.4 35.5 %copy-start = (bf16[2,24,8192]{1,2,0:T(8,128)(2,1)}, bf16[2,24,8192]{1,2,0:T(8,128)(2,1)S(1)}, u32[]{:S(2)}) copy-start(bf16[2,24,8192]{1,2,0:T(8,128)(2,1)S(1)} %pad_maximum_fusion) | copy-start | bytes 2359300
  384.6 136.4 %all-gather.3.cloned.1.call-start = ((), (), s32[]{:S(2)}) async-start(), calls=%async_computation.3 | async-start | bytes 7077888 | tf_op jit(solution)/shard_map/all_gather | solution.py:79
  423.1 254.9 %all-reduce.2.cloned.1.call-start = ((), (), s32[]{:S(2)}) async-start(), calls=%async_computation.5 | async-start | bytes 4718592 | tf_op jit(solution)/shard_map/psum | solution.py:91
Sparse Core Ops, SparseCore 0:
  384.7 8.8 all-gather.4
  423.2 97.7 all-gather.2
  580.7 97.1 all-reduce.1
where the time goes:
time: 696 us; the launch traced here: 687 us
  waiting for transfers between devices  253 us (36%)
  local copies, waits for them, and re-layouts  251 us (36%)
  matrix products  112 us (16%)
  blocking collectives  40.2 us (6%)
  between operations  13.7 us (2%)
  other arithmetic  9.75 us (1%)
  starting transfers between devices  7.67 us (1%)
    psum x1, waiting for transfers between devices, shards(): summed = lax.psum(partial_terms, ('row', 'col'))  97.4 us
    all_gather x1, waiting for transfers between devices, shards(): lax.all_gather(halves, 'row', axis=1, tiled=True)  96.3 us
    all_to_all x1, waiting for transfers between devices, shards(): lax.all_to_all(density, ('row', 'col'), split_axis=0, concat_axis=1, tile...  59.1 us
    another operation x2, local copies, waits for them, and re-layouts, shards(): rho = jnp.stack([rho_real, rho_imag], axis=0).astype(jnp.bfloat16)  45.7 us
    all_to_all x1, blocking collectives, shards(): blocks = lax.all_to_all(rho, 'row', split_axis=2, concat_axis=1, tiled=True)  35.8 us
    gather x1, local copies, waits for them, and re-layouts, shards(): jnp.take(imag_part.reshape(owned, -1), gmap, axis=1) * norm_factor  33.6 us
    gather x1, local copies, waits for them, and re-layouts, shards(): jnp.take(real_part.reshape(owned, -1), gmap, axis=1) * norm_factor  33.6 us
    unnamed x15, local copies, waits for them, and re-layouts  29 us
  transfers between devices with their start and end apart: 4, of which 3 were waited for; matrix products, arithmetic and copies ran while one was open for 5% of the time, Pallas kernels for 0%

commit v1 on v0

--- a/solution.py
+++ b/solution.py
@@ -8,6 +8,11 @@
 GX = 32
 NG = 8192
 NP = 384
+
+
+def gather_blocks(block, name, dim):
+    pieces = lax.all_gather(block, name)
+    return jnp.concatenate(pieces, axis=dim)
 
 
 def line_tables(side_len):
@@ -76,7 +81,7 @@
     rho = jnp.stack([rho_real, rho_imag], axis=0).astype(jnp.bfloat16)
     row_span = screened.shape[2]
     halves = lax.all_to_all(rho, "col", split_axis=2, concat_axis=1, tiled=True)
-    screened_rho = right_columns(screened, lax.all_gather(halves, "row", axis=1, tiled=True))
+    screened_rho = right_columns(screened, gather_blocks(halves, "row", 1))
     blocks = lax.all_to_all(rho, "row", split_axis=2, concat_axis=1, tiled=True)
     blocks = blocks.reshape(2, lax.axis_size("row"), owned, row_span)
     left_panel = lax.all_gather(blocks, "col", axis=2, tiled=True).reshape(2, NP, row_span)

time: 696 us -> 697 us (level)
  no operation moved by 1% of the time
where the time goes in v1:
time: 697 us; the launch traced here: 688 us
  local copies, waits for them, and re-layouts  255 us (37%)
  waiting for transfers between devices  253 us (36%)
  matrix products  109 us (16%)
  blocking collectives  40.1 us (6%)
  between operations  13.6 us (2%)
  other arithmetic  9.52 us (1%)
  starting transfers between devices  7.67 us (1%)
    psum x1, waiting for transfers between devices, shards(): summed = lax.psum(partial_terms, ('row', 'col'))  97.4 us
    all_gather x1, waiting for transfers between devices, gather_blocks(): pieces = lax.all_gather(block, name)  96.3 us
    all_to_all x1, waiting for transfers between devices, shards(): lax.all_to_all(density, ('row', 'col'), split_axis=0, concat_axis=1, tile...  59.1 us
    another operation x2, local copies, waits for them, and re-layouts, shards(): rho = jnp.stack([rho_real, rho_imag], axis=0).astype(jnp.bfloat16)  45.7 us
    all_to_all x1, blocking collectives, shards(): blocks = lax.all_to_all(rho, 'row', split_axis=2, concat_axis=1, tiled=True)  35.8 us
    gather x1, local copies, waits for them, and re-layouts, shards(): jnp.take(real_part.reshape(owned, -1), gmap, axis=1) * norm_factor  33.5 us
    gather x1, local copies, waits for them, and re-layouts, shards(): jnp.take(imag_part.reshape(owned, -1), gmap, axis=1) * norm_factor  33.5 us
    unnamed x15, local copies, waits for them, and re-layouts  29 us
  transfers between devices with their start and end apart: 4, of which 3 were waited for; matrix products, arithmetic and copies ran while one was open for 5% of the time, Pallas kernels for 0%

profile of v1, /device:TPU:0, one launch (start us, length us, event | category | flops | bytes accessed | tf_op | source)
XLA Modules:
  0.0 688.2 jit_solution(820082696855232240)
XLA Ops:
  6.5 0.8 slice_reduce_fusion
  7.3 1.0 copy.93
  8.3 1.4 fusion.54
  9.8 1.5 convolution_multiply_fusion
  11.3 3.8 reshape.44
  15.1 7.5 %all-to-all-start = ((f32[384,2,1024]{2,1,0:T(2,128)}), f32[384,2,1024]{2,1,0:T(2,128)S(1)}, u32[]{:S(2)}, u32[]{:S(2)}) async-start(f32[384,2,1024]{2,1,0:T(2,128)} %reshape.44), calls=%async_computation | async-start | bytes 6291456 | tf_op jit(solution)/shard_map/all_to_all | solution.py:74
  22.6 0.0 all-gather.5.cloned.1.call-start
  22.7 0.0 copy-done.4
  22.7 59.1 %all-to-all-done = f32[384,2,1024]{2,1,0:T(2,128)S(1)} async-done(((f32[384,2,1024]{2,1,0:T(2,128)}), f32[384,2,1024]{2,1,0:T(2,128)S(1)}, u32[]{:S(2)}, u32[]{:S(2)}) %all-to-all-start) | async-done | bytes 3145760 | tf_op jit(solution)/shard_map/all_to_all | solution.py:74
  81.8 1.0 copy.70
  82.9 2.4 copy.71
  85.3 7.5 %reshape.45 = f32[768,32,32]{2,1,0:T(8,128)} reshape(f32[24,16,2,1024]{3,2,1,0:T(2,128)S(1)} %copy.71) | data formatting | bytes 6291456 | tf_op jit(solution)/shard_map/reshape | solution.py:28
  92.8 9.5 %copy.72 = f32[768,32,32]{0,2,1:T(8,128)S(1)} copy(f32[768,32,32]{2,1,0:T(8,128)} %reshape.45) | data formatting | bytes 6291456 | tf_op jit(solution)/shard_map/reshape | solution.py:28
  102.3 3.0 convolution_negate_fusion
  105.4 3.0 fusion.72
  108.4 4.9 fusion.22
  113.3 5.1 fusion.24
  118.4 6.7 add_bitcast_fusion.1
  125.2 5.3 subtract_bitcast_fusion.1
  130.5 10.6 %copy.79 = f32[768,32,32]{2,1,0:T(8,128)} copy(f32[768,32,32]{0,1,2:T(8,128)S(1)} %subtract_bitcast_fusion.1) | data formatting | bytes 6291456 | tf_op jit(solution)/shard_map/sub | solution.py:34
  141.1 9.4 %reshape.47 = f32[24,32,1024]{2,1,0:T(8,128)S(1)} reshape(f32[768,32,32]{2,1,0:T(8,128)} %copy.79) | data formatting | bytes 6291456 | tf_op jit(solution)/shard_map/reshape | solution.py:37
  150.4 5.5 fusion.66
  155.9 11.4 %copy.76 = f32[768,32,32]{2,1,0:T(8,128)} copy(f32[768,32,32]{0,1,2:T(8,128)} %add_bitcast_fusion.1) | data formatting | bytes 6291456 | tf_op jit(solution)/shard_map/add | solution.py:31
  167.3 10.9 %reshape.46 = f32[24,32,1024]{2,1,0:T(8,128)} reshape(f32[768,32,32]{2,1,0:T(8,128)} %copy.76) | data formatting | bytes 6291456 | tf_op jit(solution)/shard_map/reshape | solution.py:37
  178.3 5.9 fusion.69
  184.3 5.5 subtract_bitcast_fusion
  189.8 5.6 add_bitcast_fusion
  195.4 10.2 %copy.89 = f32[24,32,1024]{0,2,1:T(8,128)} copy(f32[24,32,1024]{2,1,0:T(8,128)} %add_bitcast_fusion) | data formatting | bytes 6291456 | tf_op jit(solution)/shard_map/reshape | solution.py:79
  205.6 8.5 %copy.90 = f32[24,32,1024]{0,2,1:T(8,128)} copy(f32[24,32,1024]{2,1,0:T(8,128)S(1)} %copy-done.2) | data formatting | bytes 6291456 | tf_op jit(solution)/shard_map/reshape | solution.py:80
  214.2 33.5 %gather_fusion = f32[8192,24]{1,0:T(8,128)} fusion(f32[24,32768]{0,1:T(8,128)} %bitcast.141, s32[8192]{0:T(1024)S(1)} %fusion.57), kind=kCustom, calls=%fused_computation.clone | custom fusion | bytes 1605632 | tf_op jit(solution)/shard_map/jit(_take)/gather | solution.py:79
  247.7 33.5 %gather_fusion.1 = f32[8192,24]{1,0:T(8,128)} fusion(f32[24,32768]{0,1:T(8,128)} %bitcast.140, s32[8192]{0:T(1024)S(1)} %fusion.57), kind=kCustom, calls=%fused_computation.1.clone | custom fusion | bytes 1605632 | tf_op jit(solution)/shard_map/jit(_take)/gather | solution.py:80
  281.1 6.9 %fusion.30 = (bf16[1,24,8192]{1,2,0:T(8,128)(2,1)S(1)}, bf16[1,24,8192]{1,2,0:T(8,128)(2,1)S(1)}) fusion(f32[8192,24]{1,0:T(8,128)} %gather_fusion, pred[8192]{0:T(1024)(128)(4,1)S(1)} %compare_and_fusion, f32[8192,24]{1,0:T(8,128)} %gather_fusion.1), kind=kLoop, calls=%fused_computation.41 | loop fusion | flops 1179648 | bytes 2367488 | tf_op jit(solution)/shard_map/stack | solution.py:81
  288.1 0.9 pad_maximum_fusion
  289.0 35.5 %copy.108 = bf16[2,24,8192]{1,0,2:T(2,128)(2,1)} copy(bf16[2,24,8192]{1,2,0:T(8,128)(2,1)S(1)} %pad_maximum_fusion) | data formatting | bytes 1572864 | tf_op jit(solution)/shard_map/stack | solution.py:81
  324.5 6.6 reshape.81
  331.1 35.8 %all_to_all.45 = bf16[8,2,24576]{2,1,0:T(2,128)(2,1)S(1)} all-to-all(bf16[8,2,24576]{2,1,0:T(2,128)(2,1)S(1)} %reshape.81), channel_id=1, replica_groups=mesh['kpt'=2,'row'=8,'col'=2] {'row'}, dimensions={0} | all-to-all | bytes 1572864 | tf_op jit(solution)/shard_map/all_to_all | solution.py:85
  366.9 6.9 %reshape.82 = bf16[8192,2,24]{2,1,0:T(2,128)(2,1)} reshape(bf16[8,2,24576]{2,1,0:T(2,128)(2,1)S(1)} %all_to_all.45) | data formatting | bytes 1572864
  373.9 10.3 %copy.87 = bf16[2,24,8,1024]{3,1,2,0:T(8,128)(2,1)} copy(bf16[2,24,8,1024]{1,0,3,2:T(2,128)(2,1)} %bitcast.142) | data formatting | bytes 1572864 | tf_op jit(solution)/shard_map/all_to_all | solution.py:85
  384.2 0.0 all-gather.5.cloned.1.call-update
  384.2 0.0 all-gather.3.cloned.1.call-start
  384.2 10.2 %copy.109 = bf16[2,24,8192]{1,0,2:T(2,128)(2,1)} copy(bf16[2,24,8192]{1,2,0:T(8,128)(2,1)} %copy-done) | data formatting | bytes 1572864 | tf_op jit(solution)/shard_map/stack | solution.py:81
  394.4 7.0 %reshape.83 = bf16[2,2,98304]{2,1,0:T(2,128)(2,1)S(1)} reshape(bf16[8192,2,24]{2,1,0:T(2,128)(2,1)} %bitcast.144) | data formatting | bytes 1572864
  401.5 4.4 all_to_all.46
  405.8 7.3 %reshape.84 = bf16[8192,2,24]{2,1,0:T(2,128)(2,1)} reshape(bf16[2,2,98304]{2,1,0:T(2,128)(2,1)S(1)} %all_to_all.46) | data formatting | bytes 1572864
  413.1 9.4 %copy.83 = bf16[2,2,24,4096]{3,2,1,0:T(8,128)(2,1)} copy(bf16[2,2,24,4096]{2,0,3,1:T(2,128)(2,1)} %bitcast.143) | data formatting | bytes 1572864 | tf_op jit(solution)/shard_map/all_to_all | solution.py:83
  422.6 0.0 all-gather.3.cloned.1.call-update
  422.6 0.0 all-reduce.2.cloned.1.call-start
  422.7 0.0 all-gather.5.cloned.1.call-done
  422.7 1.5 fusion.130
  424.2 96.3 %all-gather.3.cloned.1.call-done = bf16[8,2,48,4096]{3,2,0,1:T(8,128)(2,1)} async-done(((bf16[1,2,48,4096]{3,2,0,1:T(8,128)(2,1)}), bf16[8,2,48,4096]{3,2,0,1:T(8,128)(2,1)}) %all-gather.3.cloned.1.call-update) | async-done | bytes 6291472 | tf_op jit(solution)/shard_map/all_gather | solution.py:14
  520.5 3.6 fusion.129
  524.2 11.9 %fusion = f32[384,2,1024]{2,0,1:T(8,128)} fusion(bf16[384,4096,1]{1,0,2:T(8,128)(2,1)S(1)} %bitcast.154, bf16[2,2,1024,4096]{3,2,1,0:T(8,128)(2,1)} %param.9), kind=kOutput, calls=%fused_computation.2 | convolution fusion | flops 6442450944 | bytes 23068672 | tf_op jit(solution)/shard_map/fgh,bh->fgb/dot_general | solution.py:58
  536.1 11.5 %fusion.2 = f32[384,2,1024]{2,0,1:T(8,128)} fusion(bf16[384,4096,1]{1,0,2:T(8,128)(2,1)S(1)} %bitcast.156, bf16[2,2,1024,4096]{3,2,1,0:T(8,128)(2,1)} %param.9), kind=kOutput, calls=%fused_computation.4 | convolution fusion | flops 6442450944 | bytes 23068672 | tf_op jit(solution)/shard_map/fgh,bh->fgb/dot_general | solution.py:56
  547.6 10.9 %fusion.39 = f32[384,2,1024]{2,0,1:T(8,128)S(1)} fusion(f32[384,2,1024]{2,0,1:T(8,128)} %fusion, bf16[384,4096,1]{1,0,2:T(8,128)(2,1)S(1)} %bitcast.157, bf16[2,2,1024,4096]{3,2,1,0:T(8,128)(2,1)} %param.9), kind=kOutput, calls=%fused_computation.45 | convolution fusion | flops 6443237376 | bytes 26214400 | tf_op jit(solution)/shard_map/fgh,bh->fgb/dot_general | solution.py:57
  558.4 10.9 %fusion.36 = f32[384,2,1024]{2,0,1:T(8,128)S(1)} fusion(f32[384,2,1024]{2,0,1:T(8,128)} %fusion.2, bf16[384,4096,1]{1,0,2:T(8,128)(2,1)S(1)} %bitcast.155, bf16[2,2,1024,4096]{3,2,1,0:T(8,128)(2,1)} %param.9), kind=kOutput, calls=%fused_computation.44 | convolution fusion | flops 6443237376 | bytes 26214400 | tf_op jit(solution)/shard_map/fgh,bh->fgb/dot_general | solution.py:55
  569.4 2.6 fusion.14
  572.0 2.6 fusion.16
  574.6 2.6 fusion.48
  577.2 2.6 fusion.51
  579.8 1.6 maximum_multiply_fusion
  581.4 0.0 all-reduce.2.cloned.1.call-update
  581.4 97.4 %all-reduce.2.cloned.1.call-done = f32[2,2,384,384]{2,3,0,1:T(8,128)} async-done(((f32[2,2,384,384]{2,3,0,1:T(8,128)}), f32[2,2,384,384]{2,3,0,1:T(8,128)}) %all-reduce.2.cloned.1.call-update) | async-done | bytes 2359312 | tf_op jit(solution)/shard_map/psum | solution.py:96
  678.9 1.7 constant_dynamic-slice_fusion
  680.5 0.9 copy.88
  (11 shorter events, 0.0 us)
Async XLA Ops:
  15.1 7.6 %copy-start.4 = (s32[8192]{0:T(1024)S(1)}, s32[8192]{0:T(1024)}, u32[]{:S(2)}) copy-start(s32[8192]{0:T(1024)} %param.8) | copy-start | bytes 98308
  15.1 66.8 %all-to-all-start = ((f32[384,2,1024]{2,1,0:T(2,128)}), f32[384,2,1024]{2,1,0:T(2,128)S(1)}, u32[]{:S(2)}, u32[]{:S(2)}) async-start(f32[384,2,1024]{2,1,0:T(2,128)} %reshape.44), calls=%async_computation | async-start | bytes 6291456 | tf_op jit(solution)/shard_map/all_to_all | solution.py:74
  22.6 400.1 %all-gather.5.cloned.1.call-start = ((), (), s32[]{:S(2)}) async-start(), calls=%async_computation.4 | async-start | bytes 2359296 | tf_op jit(solution)/shard_map/all_gather | solution.py:87
  178.3 6.0 copy-start.1
  178.3 6.0 copy-start.3
  195.4 10.2 %copy-start.2 = (f32[24,32,1024]{2,1,0:T(8,128)S(1)}, f32[24,32,1024]{2,1,0:T(8,128)}, u32[]{:S(2)}) copy-start(f32[24,32,1024]{2,1,0:T(8,128)} %subtract_bitcast_fusion) | copy-start | bytes 9437188
  289.0 35.5 %copy-start = (bf16[2,24,8192]{1,2,0:T(8,128)(2,1)}, bf16[2,24,8192]{1,2,0:T(8,128)(2,1)S(1)}, u32[]{:S(2)}) copy-start(bf16[2,24,8192]{1,2,0:T(8,128)(2,1)S(1)} %pad_maximum_fusion) | copy-start | bytes 2359300
  384.2 136.3 %all-gather.3.cloned.1.call-start = ((), (), s32[]{:S(2)}) async-start(), calls=%async_computation.3 | async-start | bytes 7077888 | tf_op jit(solution)/shard_map/all_gather | solution.py:14
  422.6 256.3 %all-reduce.2.cloned.1.call-start = ((), (), s32[]{:S(2)}) async-start(), calls=%async_computation.5 | async-start | bytes 4718592 | tf_op jit(solution)/shard_map/psum | solution.py:96
Sparse Core Ops, SparseCore 0:
  384.3 8.8 all-gather.4
  422.7 97.7 all-gather.2
  581.5 97.2 all-reduce.1
